TPU v7x, 256 devices: a whole 4x4x8 slice. The times are simulated.
256 devices in a mesh: row: 32 (over x_lo, z, core), col: 8 (over x_hi, y).
Axes of the slice: x: 4 (x_hi: 2, x_lo: 2; x = x_hi * 2 + x_lo), y: 4, z: 8, core: 2. Of those that a mesh axis runs over, the one named last changes fastest.
Arguments:
- joined: bfloat16 [2, 32, 32, 28, 4096], P(None, None, 'row', None, 'col'), may hold values from -0.09375 to 0.09375
- probes: bfloat16 [2, 128, 4096], P(None, None, 'col'), may hold values from -6 to 6
Outputs:
- gate_rows: bfloat16 [2, 14336, 4096], P(None, 'row', 'col')
- up_rows: bfloat16 [2, 14336, 4096], P(None, 'row', 'col')
- hidden: bfloat16 [2, 128, 14336], P(None, 'col', 'row')
All inputs are finite; a program needn't handle non-finite values.
Results may differ from a plain program's by a relative error of at most 0.002.
Values may be sent and summed in bfloat16 or wider, within the bound.
A program may use at most 64 MiB of HBM per device.

v0:
```python
import jax
import jax.numpy as jnp
from jax import lax
from jax.sharding import Mesh
from jax.sharding import PartitionSpec as P

COL = ("col_0", "col_1")


def sum_in_order(parts, axes, turns):
    inside = parts.shape[1:]
    parts = parts.reshape(*(lax.axis_size(a) for a in axes), *inside)
    parts = jnp.moveaxis(parts, turns, range(len(axes))).reshape(-1, *inside)
    for k in turns:
        parts = lax.psum_scatter(parts, axes[k], scatter_dimension=0, tiled=True)
    return parts[0]


def in_blocks(array, dim, devices):
    return jnp.stack(jnp.split(array, devices, axis=dim))


def sum_by_axis(array, axes, turns, dim):
    devices = lax.axis_size(axes)
    return sum_in_order(in_blocks(array, dim, devices), axes, turns)


def own_rows(product, extent, axes, turns):
    so_far = product(jnp.int32(0), extent * lax.axis_size(axes))
    return sum_by_axis(so_far, axes, turns, 0)


def make_term(probe_layer, gate_layer, up_layer):

    def partial_term(first_row, row_count):
        probe_rows = lax.dynamic_slice_in_dim(probe_layer, first_row, row_count, 0)
        gate_part = jnp.dot(probe_rows, gate_layer.T, preferred_element_type=jnp.float32)
        up_part = jnp.dot(probe_rows, up_layer.T, preferred_element_type=jnp.float32)
        return jnp.concatenate((gate_part, up_part), axis=1)

    return partial_term


def body(joined, probes):
    layers = joined.shape[0]
    cycles = joined.shape[1]
    block_rows = joined.shape[3]
    columns = joined.shape[4]
    peer_count = lax.axis_size("row")
    groups = cycles // peer_count
    half_rows = block_rows // 2
    outgoing = joined.reshape(layers, peer_count, groups, block_rows, columns)
    arrived = lax.all_to_all(outgoing, "row", split_axis=1, concat_axis=1, tiled=True)
    separated = arrived.reshape(layers, peer_count, groups, half_rows, 2, columns)
    rows_own = peer_count * groups * half_rows
    gate_rows = (
        separated[:, :, :, :, 0, :].transpose(0, 2, 1, 3, 4).reshape(layers, rows_own, columns)
    )
    up_rows = (
        separated[:, :, :, :, 1, :].transpose(0, 2, 1, 3, 4).reshape(layers, rows_own, columns)
    )
    row_share = probes.shape[1] // lax.axis_size(COL)
    results = []
    for layer_index in range(layers):
        partial_term = make_term(probes[layer_index], gate_rows[layer_index], up_rows[layer_index])
        summed = own_rows(partial_term, row_share, COL, (1, 0))
        results.append(
            (jax.nn.silu(summed[:, :rows_own]) * summed[:, rows_own:]).astype(jnp.bfloat16)
        )
    hidden = jnp.stack(results, axis=0)
    return (gate_rows, up_rows, hidden)


def solution(mesh):
    split = Mesh(mesh.devices.reshape(mesh.shape["row"], 2, 4), ("row", "col_0", "col_1"))
    return jax.shard_map(
        body,
        mesh=split,
        in_specs=(P(None, None, "row", None, COL), P(None, None, COL)),
        out_specs=(P(None, "row", COL), P(None, "row", COL), P(None, COL, "row")),
        check_vma=False,
    )
```

profile of v0, /device:TPU:1, one launch (start us, length us, event | category | flops | bytes accessed | tf_op | source)
XLA Modules:
  0.0 193.5 jit_solution(3140879627541068802)
XLA Ops:
  7.2 2.5 %copy.46 = bf16[2,32,1,28,512]{4,3,2,0,1:T(8,128)(2,1)S(1)} copy(bf16[2,32,1,28,512]{4,1,3,2,0:T(8,128)(2,1)} %param.2) | data formatting | bytes 3670016 | tf_op args[0]
  9.7 59.7 %all_to_all.5 = bf16[2,32,1,28,512]{4,3,2,0,1:T(8,128)(2,1)S(1)} all-to-all(bf16[2,32,1,28,512]{4,3,2,0,1:T(8,128)(2,1)S(1)} %copy.46), channel_id=1, replica_groups=mesh['row'=32,'col_0'=2,'col_1'=4] {'row'}, dimensions={1} | all-to-all | bytes 3670016 | tf_op jit(solution)/shard_map/all_to_all | solution.py:53
  69.4 1.0 copy.47
  70.4 0.9 fusion.46
  71.6 0.9 squeeze.26
  72.5 1.3 copy.62
  73.8 0.9 squeeze.30
  74.7 2.0 %fusion.34 = f32[128,448]{0,1:T(8,128)} fusion(bf16[448,512]{1,0:T(8,128)(2,1)} %squeeze.26, bf16[2,128,512]{2,1,0:T(8,128)(2,1)S(1)} %copy-done), kind=kOutput, calls=%fused_computation.64 | convolution fusion | flops 58720256 | bytes 819200 | tf_op jit(solution)/shard_map/dot_general | solution.py:38
  76.7 2.0 %fusion.30 = f32[128,448]{0,1:T(8,128)} fusion(bf16[448,512]{1,0:T(8,128)(2,1)} %squeeze.30, bf16[2,128,512]{2,1,0:T(8,128)(2,1)S(1)} %copy-done), kind=kOutput, calls=%fused_computation.60 | convolution fusion | flops 58720256 | bytes 819200 | tf_op jit(solution)/shard_map/dot_general | solution.py:38
  79.0 1.0 fusion.32
  80.7 4.0 %fusion.29 = (f32[1,16,896]{1,2,0:T(8,128)}, f32[1,16,896]{1,2,0:T(8,128)}, f32[1,16,896]{1,2,0:T(8,128)}, f32[1,16,896]{1,2,0:T(8,128)}, f32[1,16,896]{1,2,0:T(...) fusion(f32[128,448]{0,1:T(8,128)} %fusion.34, f32[128,448]{0,1:T(8,128)S(1)} %fusion.36), kind=kLoop, calls=%fused_computation.59 | loop fusion | flops 114688 | bytes 917504 | tf_op jit(solution)/shard_map/stack | solution.py:20
  84.7 1.2 copy.59
  85.9 1.8 copy.52
  87.7 1.8 copy.53
  89.6 1.8 copy.54
  91.4 1.8 copy.55
  97.9 4.0 %fusion.28 = (f32[1,16,896]{1,2,0:T(8,128)}, f32[1,16,896]{1,2,0:T(8,128)}, f32[1,16,896]{1,2,0:T(8,128)}, f32[1,16,896]{1,2,0:T(8,128)}, f32[1,16,896]{1,2,0:T(...) fusion(f32[128,448]{0,1:T(8,128)S(1)} %copy-done.1, f32[128,448]{0,1:T(8,128)} %fusion.32), kind=kLoop, calls=%fused_computation.57 | loop fusion | flops 114688 | bytes 917504 | tf_op jit(solution)/shard_map/stack | solution.py:20
  102.0 1.2 copy.70
  103.1 1.2 copy.63
  104.3 1.2 copy.64
  105.5 1.2 copy.65
  106.7 1.2 copy.66
  109.4 9.5 %reduce-scatter.5.cloned.1.call-done = f32[2,16,896]{2,1,0:T(8,128)} async-done(((f32[8,16,896]{2,1,0:T(8,128)}), f32[2,16,896]{2,1,0:T(8,128)}) %reduce-scatter.5.cloned.1.call-update) | async-done | bytes 114704 | tf_op jit(solution)/shard_map/reduce_scatter | solution.py:15
  119.0 26.7 %reduce-scatter.9.cloned.1.call-done = f32[2,16,896]{2,1,0:T(8,128)} async-done(((f32[8,16,896]{2,1,0:T(8,128)}), f32[2,16,896]{2,1,0:T(8,128)}) %reduce-scatter.9.cloned.1.call-update) | async-done | bytes 114704 | tf_op jit(solution)/shard_map/reduce_scatter | solution.py:15
  146.0 0.9 copy.49
  146.9 1.1 copy.73
  148.0 0.9 copy.48
  149.0 1.1 copy.72
  150.0 16.8 %reduce-scatter.7.cloned.1.call-done = f32[1,16,896]{2,1,0:T(8,128)} async-done(((f32[2,16,896]{2,1,0:T(8,128)}), f32[1,16,896]{2,1,0:T(8,128)}) %reduce-scatter.7.cloned.1.call-update) | async-done | bytes 57360 | tf_op jit(solution)/shard_map/reduce_scatter | solution.py:15
  166.8 0.9 fusion.44
  167.7 17.7 %reduce-scatter.11.cloned.1.call-done = f32[1,16,896]{2,1,0:T(8,128)} async-done(((f32[2,16,896]{2,1,0:T(8,128)}), f32[1,16,896]{2,1,0:T(8,128)}) %reduce-scatter.11.cloned.1.call-update) | async-done | bytes 57360 | tf_op jit(solution)/shard_map/reduce_scatter | solution.py:15
  185.4 0.9 fusion.45
  (44 shorter events, 8.4 us)
Async XLA Ops:
  7.2 111.8 %reduce-scatter.5.cloned.1.call-start = ((), (), s32[]{:S(2)}) async-start(), calls=%async_computation.5 | async-start | bytes 573440 | tf_op jit(solution)/shard_map/reduce_scatter | solution.py:15
  71.3 3.3 %copy-start = (bf16[2,128,512]{2,1,0:T(8,128)(2,1)S(1)}, bf16[2,128,512]{2,1,0:T(8,128)(2,1)}, u32[]{:S(2)}) copy-start(bf16[2,128,512]{2,1,0:T(8,128)(2,1)} %param.3) | copy-start | bytes 786436
  93.2 4.7 %copy-start.1 = (f32[128,448]{0,1:T(8,128)S(1)}, f32[128,448]{0,1:T(8,128)}, u32[]{:S(2)}) copy-start(f32[128,448]{0,1:T(8,128)} %fusion.30) | copy-start | bytes 688132
  97.9 47.9 %reduce-scatter.9.cloned.1.call-start = ((), (), s32[]{:S(2)}) async-start(), calls=%async_computation.7 | async-start | bytes 573440 | tf_op jit(solution)/shard_map/reduce_scatter | solution.py:15
  109.4 57.5 %reduce-scatter.7.cloned.1.call-start = ((), (), s32[]{:S(2)}) async-start(), calls=%async_computation.6 | async-start | bytes 172032 | tf_op jit(solution)/shard_map/reduce_scatter | solution.py:15
  119.0 66.5 %reduce-scatter.11.cloned.1.call-start = ((), (), s32[]{:S(2)}) async-start(), calls=%async_computation.8 | async-start | bytes 172032 | tf_op jit(solution)/shard_map/reduce_scatter | solution.py:15
Sparse Core Ops, SparseCore 0:
  98.0 20.9 reduce-scatter.4
  122.1 23.6 reduce-scatter.8
  148.2 18.5 reduce-scatter.6
  169.1 16.2 reduce-scatter.10
where the time goes:
time: 195 us; the launch traced here: 194 us
  waiting for transfers between devices  70.8 us (36%)
  blocking collectives  59.7 us (31%)
  local copies, waits for them, and re-layouts  33.2 us (17%)
  between operations  13.9 us (7%)
  other arithmetic  10.5 us (5%)
  matrix products  5.21 us (3%)
    reduce_scatter x4, waiting for transfers between devices, sum_in_order(): parts = lax.psum_scatter(parts, axes[k], scatter_dimension=0, tiled=True)  70.8 us
    all_to_all x1, blocking collectives, body(): lax.all_to_all(outgoing, 'row', split_axis=1, concat_axis=1, tiled=True)  59.7 us
    another operation x18, local copies, waits for them, and re-layouts, in_blocks(): return jnp.stack(jnp.split(array, devices, axis=dim))  15.4 us
    another operation x2, other arithmetic, in_blocks(): return jnp.stack(jnp.split(array, devices, axis=dim))  8.08 us
    unnamed x21, local copies, waits for them, and re-layouts  8.07 us
    dot_general x2, matrix products, partial_term(): jnp.dot(probe_rows, up_layer.T, preferred_element_type=jnp.float32)  3.96 us
  transfers between devices with their start and end apart: 4, of which 4 were waited for; matrix products, arithmetic and copies ran while one was open for 9% of the time, Pallas kernels for 0%

commit v1 on v0

v1 whole, which is shorter than its diff:
```python
import functools

import jax
import jax.numpy as jnp
from jax import lax
from jax.experimental import pallas as pl
from jax.experimental.pallas import tpu as pltpu
from jax.sharding import PartitionSpec as P

MESH = pl.DeviceIdType.MESH
L, C, R, B, W = 2, 32, 32, 28, 512
HB = B // 2
J = L * B
T = 128
NY, NX = 4, 2
TC = T // (NY * NX)
PITCH = C + 1
LANES = 128
TILES = W // LANES
HALFW = 512
ROWS = C * HB


def exchange(
    x_hbm, p_hbm, got, hid, xs, pv, spread, msg, part, in_a, summed, in_b, hidt, hsend, hgot, order,
    load_sem, p_sem, own_sem, w_send, w_recv, a_send, a_recv, b_send, b_recv, h_send, h_recv,
):
    me = lax.axis_index("row")
    col = lax.axis_index("col")
    xh, y = col // NY, col % NY

    for gu in range(2):
        for l in range(L):
            q = gu * L + l
            pltpu.make_async_copy(x_hbm.at[l, :, gu], xs.at[pl.ds(q * HB, HB)], load_sem.at[q]).start()
    pltpu.make_async_copy(p_hbm, pv, p_sem).start()

    barrier = pltpu.get_barrier_semaphore()

    def hello(i, _):
        pl.semaphore_signal(barrier, inc=1, device_id={"row": (me + i) % R}, device_id_type=MESH)
        return _

    lax.fori_loop(1, R, hello, 0)
    for dy in range(1, NY):
        pl.semaphore_signal(barrier, inc=1, device_id={"col": xh * NY + (y + dy) % NY}, device_id_type=MESH)
    partner = (1 - xh) * NY + y
    pl.semaphore_signal(barrier, inc=1, device_id={"col": partner}, device_id_type=MESH)

    for q in range(2 * L):
        pltpu.make_async_copy(x_hbm.at[q % L, :, q // L], xs.at[pl.ds(q * HB, HB)], load_sem.at[q]).wait()
        for i in range(HB):
            j = q * HB + i
            rows = xs[j].astype(jnp.float32)
            for c in range(TILES):
                spread[c, pl.ds(j * PITCH, C), :] = rows[:, c * LANES:(c + 1) * LANES]
    for k in range(C):
        for c in range(TILES):
            msg[k, :, pl.ds(c * LANES, LANES)] = spread[c, pl.ds(k, J, stride=PITCH), :].astype(jnp.bfloat16)

    pltpu.make_async_copy(p_hbm, pv, p_sem).wait()
    for l in range(L):
        for gu in range(2):
            rows = xs[pl.ds((gu * L + l) * HB, HB)].reshape(ROWS, W)
            proj = lax.dot_general(
                pv[l], rows, (((1,), (1,)), ((), ())), preferred_element_type=jnp.float32
            )
            for a in range(NX):
                for b in range(NY):
                    t = (a * NY + b) * TC
                    part[b, a, l, :, pl.ds(gu * HALFW, ROWS)] = proj[t:t + TC]

    pl.semaphore_wait(barrier, R - 1 + NY)

    def weights(i):
        to = (me + i) % R
        return pltpu.make_async_remote_copy(
            src_ref=msg.at[to], dst_ref=got.at[me], send_sem=w_send.at[i], recv_sem=w_recv.at[me],
            device_id={"row": to}, device_id_type=MESH,
        )

    def hiddens(i):
        to = (me + i) % R
        return pltpu.make_async_remote_copy(
            src_ref=hsend.at[to], dst_ref=hgot.at[me], send_sem=h_send.at[i], recv_sem=h_recv.at[me],
            device_id={"row": to}, device_id_type=MESH,
        )

    def start_weights(i, _):
        weights(i).start()
        return _

    def phase_a(dy):
        to = (y + dy) % NY
        return pltpu.make_async_remote_copy(
            src_ref=part.at[to], dst_ref=in_a.at[dy - 1], send_sem=a_send.at[dy - 1], recv_sem=a_recv.at[dy - 1],
            device_id={"col": xh * NY + to}, device_id_type=MESH,
        )

    for dy in range(1, NY):
        phase_a(dy).start()
    lax.fori_loop(1, R, start_weights, 0)
    own = pltpu.make_async_copy(msg.at[me], got.at[me], own_sem)
    own.start()

    for dy in range(1, NY):
        phase_a(dy).wait()
    summed[...] = part[y] + in_a[0] + in_a[1] + in_a[2]
    phase_b = pltpu.make_async_remote_copy(
        src_ref=summed.at[1 - xh], dst_ref=in_b, send_sem=b_send, recv_sem=b_recv,
        device_id={"col": partner}, device_id_type=MESH,
    )
    phase_b.start()
    phase_b.wait()
    total = summed[xh] + in_b[...]
    gate, up = total[:, :, :HALFW], total[:, :, HALFW:]
    act = gate / (1.0 + jnp.exp(-gate)) * up
    stacked = jnp.concatenate(
        [act[l, :, g * LANES:(g + 1) * LANES] for g in range(4) for l in range(L)], axis=0
    )
    hidt[...] = stacked.T
    for k in range(C):
        hsend[k] = hidt[pl.ds(k, 4, stride=C), :].astype(jnp.bfloat16)

    def start_hidden(i, _):
        hiddens(i).start()
        return _

    lax.fori_loop(1, R, start_hidden, 0)
    hgot[me] = hsend[me]

    def wait_hidden(i, _):
        src = (me + i) % R
        pltpu.make_async_copy(hsend.at[0], hgot.at[src], h_recv.at[src]).wait()
        return _

    for i in range(1, R):
        hiddens(i).wait_send()
    for i in range(1, R):
        src = (me + i) % R
        pltpu.make_async_remote_copy(
            src_ref=hsend.at[0], dst_ref=hgot.at[src], send_sem=h_send.at[i], recv_sem=h_recv.at[src],
            device_id={"row": src}, device_id_type=MESH,
        ).wait_recv()
    for g in (3, 0, 1, 2):
        n = 2 if g == 3 else 4
        for p in range(R):
            piece = hgot[p].astype(jnp.float32)
            order[pl.ds(p * HB + 4 * g, n), :] = pltpu.roll(piece, (LANES - 32 * g) % LANES, 1)[:n]
    flat = order[...].T
    for l in range(L):
        hid[l] = flat[l * TC:(l + 1) * TC, :ROWS].astype(jnp.bfloat16)

    own.wait()
    for i in range(1, R):
        src = (me + i) % R
        weights(i).wait_send()
        pltpu.make_async_remote_copy(
            src_ref=msg.at[0], dst_ref=got.at[src], send_sem=w_send.at[i], recv_sem=w_recv.at[src],
            device_id={"row": src}, device_id_type=MESH,
        ).wait_recv()


def arrange(got, hid_in, gate, up, hid, flat, lined):
    flat[...] = got[...].astype(jnp.float32).reshape(R * J, LANES)
    for p in range(R):
        for q in range(2 * L):
            lined[q, pl.ds(p * HB, HB), :] = flat[pl.ds(p * J + q * HB, HB), :]
    for l in range(L):
        gate[l] = lined[l].astype(jnp.bfloat16)
        up[l] = lined[L + l].astype(jnp.bfloat16)
    hid[...] = hid_in[...]


def body(joined, probes):
    x = jnp.transpose(joined, (0, 2, 3, 1, 4)).reshape(L, HB, 2, C, W)
    anywhere = pl.BlockSpec(memory_space=pl.ANY)
    dma = pltpu.SemaphoreType.DMA
    f32, bf16 = jnp.float32, jnp.bfloat16
    got, hid = pl.pallas_call(
        exchange,
        out_shape=(
            jax.ShapeDtypeStruct((R, J, W), bf16),
            jax.ShapeDtypeStruct((L, TC, ROWS), bf16),
        ),
        in_specs=[anywhere, anywhere],
        out_specs=(anywhere, pl.BlockSpec(memory_space=pltpu.VMEM)),
        scratch_shapes=[
            pltpu.VMEM((J, C, W), bf16),
            pltpu.VMEM((L, T, W), bf16),
            pltpu.VMEM((TILES, J * PITCH, LANES), f32),
            pltpu.VMEM((C, J, W), bf16),
            pltpu.VMEM((NY, NX, L, TC, 2 * HALFW), f32),
            pltpu.VMEM((NY - 1, NX, L, TC, 2 * HALFW), f32),
            pltpu.VMEM((NX, L, TC, 2 * HALFW), f32),
            pltpu.VMEM((L, TC, 2 * HALFW), f32),
            pltpu.VMEM((LANES, LANES), f32),
            pltpu.VMEM((C, 4, LANES), bf16),
            pltpu.VMEM((R, 4, LANES), bf16),
            pltpu.VMEM((512, LANES), f32),
            dma((2 * L,)), dma, dma,
            dma((R,)), dma((R,)),
            dma((NY - 1,)), dma((NY - 1,)),
            dma, dma,
            dma((R,)), dma((R,)),
        ],
        compiler_params=pltpu.CompilerParams(
            collective_id=0, has_side_effects=True, vmem_limit_bytes=32 * 2**20
        ),
        name="exchange",
    )(x, probes)
    gate, up, hidden = pl.pallas_call(
        arrange,
        grid=(TILES,),
        out_shape=(
            jax.ShapeDtypeStruct((L, ROWS, W), bf16),
            jax.ShapeDtypeStruct((L, ROWS, W), bf16),
            jax.ShapeDtypeStruct((L, TC, ROWS), bf16),
        ),
        in_specs=[
            pl.BlockSpec((R, J, LANES), lambda c: (0, 0, c)),
            pl.BlockSpec((L, TC, ROWS), lambda c: (0, 0, 0)),
        ],
        out_specs=(
            pl.BlockSpec((L, ROWS, LANES), lambda c: (0, 0, c)),
            pl.BlockSpec((L, ROWS, LANES), lambda c: (0, 0, c)),
            pl.BlockSpec((L, TC, ROWS), lambda c: (0, 0, 0)),
        ),
        scratch_shapes=[
            pltpu.VMEM((R * J, LANES), f32),
            pltpu.VMEM((2 * L, ROWS, LANES), f32),
        ],
        name="arrange",
    )(got, hid)
    return gate, up, hidden


def solution(mesh):
    return jax.shard_map(
        body,
        mesh=mesh,
        in_specs=(P(None, None, "row", None, "col"), P(None, None, "col")),
        out_specs=(P(None, "row", "col"), P(None, "row", "col"), P(None, "col", "row")),
        check_vma=False,
    )
```

time: 195 us -> 65 us (0.33)
  waiting for transfers between devices: 70.8 us -> 0 us
  Pallas kernels: 0 us -> 59.8 us
  blocking collectives: 59.7 us -> 0 us
  local copies, waits for them, and re-layouts: 33.2 us -> 4.31 us
  between operations: 13.9 us -> 0.66 us
  other arithmetic: 10.5 us -> 0 us
  matrix products: 5.21 us -> 0 us
    reduce_scatter x4 -> x0, waiting for transfers between devices: 70.8 us -> none  [sum_in_order(): parts = lax.psum_scatter(parts, axes[k], scatter_dimension=0, tiled=True)]
    pallas_call x0 -> x2, Pallas kernels: none -> 59.8 us  [the longest x1 55.9 us: body(): pl.pallas_call(exchange, out_shape=(jax.ShapeDtypeStruct((R, J, W), bf16)...]
    all_to_all x1 -> x0, blocking collectives: 59.7 us -> none  [body(): lax.all_to_all(outgoing, 'row', split_axis=1, concat_axis=1, tiled=True)]
    another operation x18 -> x0, local copies, waits for them, and re-layouts: 15.4 us -> none  [in_blocks(): return jnp.stack(jnp.split(array, devices, axis=dim))]
    another operation x5 -> x0, other arithmetic: 10.5 us -> none  [the longest x2 8.08 us: in_blocks(): return jnp.stack(jnp.split(array, devices, axis=dim))]
    dot_general x4 -> x0, matrix products: 5.21 us -> none  [the longest x2 3.96 us: partial_term(): jnp.dot(probe_rows, up_layer.T, preferred_element_type=jnp.float32)]
    slice x8 -> x0, local copies, waits for them, and re-layouts: 5.06 us -> none  [the longest x3 2.45 us: body(): up_rows[layer_index]]
    unnamed x21 -> x8, local copies, waits for them, and re-layouts: 8.07 us -> 4.31 us
  transfers between devices with their start and end apart: 4 -> 0, of which waited for: 4 -> 0; matrix products, arithmetic and copies ran while one was open for 9% -> 0% of each run, Pallas kernels for 0% -> 0%
where the time goes in v1:
time: 65 us; the launch traced here: 64.7 us
  Pallas kernels  59.8 us (92%)
  local copies, waits for them, and re-layouts  4.31 us (7%)
  between operations  0.66 us (1%)
    pallas_call x1, Pallas kernels, body(): pl.pallas_call(exchange, out_shape=(jax.ShapeDtypeStruct((R, J, W), bf16)...  55.9 us
    unnamed x8, local copies, waits for them, and re-layouts  4.31 us
    pallas_call x1, Pallas kernels, body(): pl.pallas_call(arrange, grid=(TILES,), out_shape=(jax.ShapeDtypeStruct((L...  3.9 us

profile of v1, /device:TPU:1, one launch (start us, length us, event | category | flops | bytes accessed | tf_op | source)
XLA Modules:
  0.0 64.7 jit_solution(6395677573370641286)
XLA Ops:
  0.6 0.0 copy-start.1
  0.6 1.5 %copy-done.1 = bf16[2,32,1,28,512]{4,1,3,2,0:T(8,128)(2,1)S(1)} copy-done((bf16[2,32,1,28,512]{4,1,3,2,0:T(8,128)(2,1)S(1)}, bf16[2,32,1,28,512]{4,1,3,2,0:T(8,128)(2,1)}, u32[]{:S(2)}) %copy-start.1) | copy-done | bytes 1835032
  2.1 0.0 copy-start.2
  2.1 0.9 %copy-done.2 = bf16[2,128,512]{2,1,0:T(8,128)(2,1)S(1)} copy-done((bf16[2,128,512]{2,1,0:T(8,128)(2,1)S(1)}, bf16[2,128,512]{2,1,0:T(8,128)(2,1)}, u32[]{:S(2)}) %copy-start.2) | copy-done | bytes 262168
  3.1 55.9 %exchange.1 = (bf16[32,56,512]{2,1,0:T(8,128)(2,1)S(1)}, bf16[2,16,448]{2,1,0:T(8,128)(2,1)S(1)}) custom-call(bf16[2,14,2,32,512]{4,3,2,1,0:T(8,128)(2,1)S(1)} %bitcast.3, bf16[2,128,512]{2,1,0:T(8,128)(2,1)S(1)} %copy-done.2), custom_call_target="tpu_custom_call" | custom-call | tf_op jit(solution)/shard_map/exchange/pallas_call | solution.py:180
  59.0 0.0 copy-start
  59.0 1.2 %copy-done = bf16[32,56,512]{2,1,0:T(8,128)(2,1)} copy-done((bf16[32,56,512]{2,1,0:T(8,128)(2,1)}, bf16[32,56,512]{2,1,0:T(8,128)(2,1)S(1)}, u32[]{:S(2)}) %copy-start) | copy-done | bytes 1835032
  60.2 0.0 copy-start.3
  60.2 0.6 copy-done.3
  60.8 3.9 %arrange.1 = (bf16[2,448,512]{2,1,0:T(8,128)(2,1)}, bf16[2,448,512]{2,1,0:T(8,128)(2,1)}, bf16[2,16,448]{2,1,0:T(8,128)(2,1)}) custom-call(bf16[32,56,512]{2,1,0:T(8,128)(2,1)} %copy-done, bf16[2,16,448]{2,1,0:T(8,128)(2,1)} %copy-done.3), custom_call_target="tpu_custom_call" | custom-call | tf_op jit(solution)/shard_map/arrange/pallas_call | solution.py:212
Async XLA Ops:
  0.6 1.5 %copy-start.1 = (bf16[2,32,1,28,512]{4,1,3,2,0:T(8,128)(2,1)S(1)}, bf16[2,32,1,28,512]{4,1,3,2,0:T(8,128)(2,1)}, u32[]{:S(2)}) copy-start(bf16[2,32,1,28,512]{4,1,3,2,0:T(8,128)(2,1)} %param.2) | copy-start | bytes 5505028
  2.1 0.9 %copy-start.2 = (bf16[2,128,512]{2,1,0:T(8,128)(2,1)S(1)}, bf16[2,128,512]{2,1,0:T(8,128)(2,1)}, u32[]{:S(2)}) copy-start(bf16[2,128,512]{2,1,0:T(8,128)(2,1)} %p_hbm.1) | copy-start | bytes 786436
  59.0 1.3 %copy-start = (bf16[32,56,512]{2,1,0:T(8,128)(2,1)}, bf16[32,56,512]{2,1,0:T(8,128)(2,1)S(1)}, u32[]{:S(2)}) copy-start(bf16[32,56,512]{2,1,0:T(8,128)(2,1)S(1)} %get-tuple-element.5.got) | copy-start | bytes 5505028
  60.2 0.6 copy-start.3

commit v2 on v1

--- a/solution.py
+++ b/solution.py
@@ -22,8 +22,8 @@
 
 
 def exchange(
-    x_hbm, p_hbm, got, hid, xs, pv, spread, msg, part, in_a, summed, in_b, hidt, hsend, hgot, order,
-    load_sem, p_sem, own_sem, w_send, w_recv, a_send, a_recv, b_send, b_recv, h_send, h_recv,
+    x_hbm, p_hbm, gate, up, hid, xs, pv, spread, msg, got, stage, lined, part, in_a, summed, in_b, hidt, hsend, hgot, order,
+    load_sem, p_sem, w_send, w_recv, a_send, a_recv, b_send, b_recv, h_send, h_recv,
 ):
     me = lax.axis_index("row")
     col = lax.axis_index("col")
@@ -100,8 +100,15 @@
     for dy in range(1, NY):
         phase_a(dy).start()
     lax.fori_loop(1, R, start_weights, 0)
-    own = pltpu.make_async_copy(msg.at[me], got.at[me], own_sem)
-    own.start()
+
+    def place(p, rows_of):
+        for c in range(TILES):
+            stage[c] = rows_of[p, :, pl.ds(c * LANES, LANES)].astype(jnp.float32)
+        for c in range(TILES):
+            for q in range(2 * L):
+                lined[q, c, pl.ds(p * HB, HB), :] = stage[c, pl.ds(q * HB, HB), :]
+
+    place(me, msg)
 
     for dy in range(1, NY):
         phase_a(dy).wait()
@@ -113,8 +120,8 @@
     phase_b.start()
     phase_b.wait()
     total = summed[xh] + in_b[...]
-    gate, up = total[:, :, :HALFW], total[:, :, HALFW:]
-    act = gate / (1.0 + jnp.exp(-gate)) * up
+    left, right = total[:, :, :HALFW], total[:, :, HALFW:]
+    act = left / (1.0 + jnp.exp(-left)) * right
     stacked = jnp.concatenate(
         [act[l, :, g * LANES:(g + 1) * LANES] for g in range(4) for l in range(L)], axis=0
     )
@@ -128,11 +135,6 @@
 
     lax.fori_loop(1, R, start_hidden, 0)
     hgot[me] = hsend[me]
-
-    def wait_hidden(i, _):
-        src = (me + i) % R
-        pltpu.make_async_copy(hsend.at[0], hgot.at[src], h_recv.at[src]).wait()
-        return _
 
     for i in range(1, R):
         hiddens(i).wait_send()
@@ -151,45 +153,65 @@
     for l in range(L):
         hid[l] = flat[l * TC:(l + 1) * TC, :ROWS].astype(jnp.bfloat16)
 
-    own.wait()
-    for i in range(1, R):
-        src = (me + i) % R
-        weights(i).wait_send()
+    def arrived(i, _):
+        src = (me + R - i) % R
         pltpu.make_async_remote_copy(
             src_ref=msg.at[0], dst_ref=got.at[src], send_sem=w_send.at[i], recv_sem=w_recv.at[src],
             device_id={"row": src}, device_id_type=MESH,
         ).wait_recv()
-
-
-def arrange(got, hid_in, gate, up, hid, flat, lined):
-    flat[...] = got[...].astype(jnp.float32).reshape(R * J, LANES)
-    for p in range(R):
-        for q in range(2 * L):
-            lined[q, pl.ds(p * HB, HB), :] = flat[pl.ds(p * J + q * HB, HB), :]
+        place(src, got)
+        return _
+
+    lax.fori_loop(1, R, arrived, 0)
     for l in range(L):
-        gate[l] = lined[l].astype(jnp.bfloat16)
-        up[l] = lined[L + l].astype(jnp.bfloat16)
-    hid[...] = hid_in[...]
+        for c in range(TILES):
+            gate[l, :, pl.ds(c * LANES, LANES)] = lined[l, c].astype(jnp.bfloat16)
+            up[l, :, pl.ds(c * LANES, LANES)] = lined[L + l, c].astype(jnp.bfloat16)
+
+    def sent(i, _):
+        weights(i).wait_send()
+        return _
+
+    lax.fori_loop(1, R, sent, 0)
+
+
+def emit(gate_in, up_in, hid_in, gate, up, hid, sems):
+    copies = [
+        pltpu.make_async_copy(a, b, sems.at[i])
+        for i, (a, b) in enumerate(((gate_in, gate), (up_in, up), (hid_in, hid)))
+    ]
+    for copy in copies:
+        copy.start()
+    for copy in copies:
+        copy.wait()
 
 
 def body(joined, probes):
     x = jnp.transpose(joined, (0, 2, 3, 1, 4)).reshape(L, HB, 2, C, W)
-    anywhere = pl.BlockSpec(memory_space=pl.ANY)
+    hbm = pl.BlockSpec(memory_space=pltpu.HBM)
+    vmem = pl.BlockSpec(memory_space=pltpu.VMEM)
     dma = pltpu.SemaphoreType.DMA
     f32, bf16 = jnp.float32, jnp.bfloat16
-    got, hid = pl.pallas_call(
+    outs = (
+        jax.ShapeDtypeStruct((L, ROWS, W), bf16),
+        jax.ShapeDtypeStruct((L, ROWS, W), bf16),
+        jax.ShapeDtypeStruct((L, TC, ROWS), bf16),
+    )
+    x = pltpu.with_memory_space_constraint(x, pltpu.HBM)
+    probes = pltpu.with_memory_space_constraint(probes, pltpu.HBM)
+    held = pl.pallas_call(
         exchange,
-        out_shape=(
-            jax.ShapeDtypeStruct((R, J, W), bf16),
-            jax.ShapeDtypeStruct((L, TC, ROWS), bf16),
-        ),
-        in_specs=[anywhere, anywhere],
-        out_specs=(anywhere, pl.BlockSpec(memory_space=pltpu.VMEM)),
+        out_shape=outs,
+        in_specs=[hbm, hbm],
+        out_specs=(vmem, vmem, vmem),
         scratch_shapes=[
             pltpu.VMEM((J, C, W), bf16),
             pltpu.VMEM((L, T, W), bf16),
             pltpu.VMEM((TILES, J * PITCH, LANES), f32),
             pltpu.VMEM((C, J, W), bf16),
+            pltpu.VMEM((R, J, W), bf16),
+            pltpu.VMEM((TILES, J, LANES), f32),
+            pltpu.VMEM((2 * L, TILES, ROWS, LANES), f32),
             pltpu.VMEM((NY, NX, L, TC, 2 * HALFW), f32),
             pltpu.VMEM((NY - 1, NX, L, TC, 2 * HALFW), f32),
             pltpu.VMEM((NX, L, TC, 2 * HALFW), f32),
@@ -198,7 +220,7 @@
             pltpu.VMEM((C, 4, LANES), bf16),
             pltpu.VMEM((R, 4, LANES), bf16),
             pltpu.VMEM((512, LANES), f32),
-            dma((2 * L,)), dma, dma,
+            dma((2 * L,)), dma,
             dma((R,)), dma((R,)),
             dma((NY - 1,)), dma((NY - 1,)),
             dma, dma,
@@ -209,30 +231,15 @@
         ),
         name="exchange",
     )(x, probes)
-    gate, up, hidden = pl.pallas_call(
-        arrange,
-        grid=(TILES,),
-        out_shape=(
-            jax.ShapeDtypeStruct((L, ROWS, W), bf16),
-            jax.ShapeDtypeStruct((L, ROWS, W), bf16),
-            jax.ShapeDtypeStruct((L, TC, ROWS), bf16),
-        ),
-        in_specs=[
-            pl.BlockSpec((R, J, LANES), lambda c: (0, 0, c)),
-            pl.BlockSpec((L, TC, ROWS), lambda c: (0, 0, 0)),
-        ],
-        out_specs=(
-            pl.BlockSpec((L, ROWS, LANES), lambda c: (0, 0, c)),
-            pl.BlockSpec((L, ROWS, LANES), lambda c: (0, 0, c)),
-            pl.BlockSpec((L, TC, ROWS), lambda c: (0, 0, 0)),
-        ),
-        scratch_shapes=[
-            pltpu.VMEM((R * J, LANES), f32),
-            pltpu.VMEM((2 * L, ROWS, LANES), f32),
-        ],
-        name="arrange",
-    )(got, hid)
-    return gate, up, hidden
+    return pl.pallas_call(
+        emit,
+        out_shape=outs,
+        in_specs=[vmem, vmem, vmem],
+        out_specs=(hbm, hbm, hbm),
+        scratch_shapes=[dma((3,))],
+        compiler_params=pltpu.CompilerParams(vmem_limit_bytes=2 * 2**20),
+        name="emit",
+    )(*held)
 
 
 def solution(mesh):

time: 65 us -> 59.1 us (0.909)
  local copies, waits for them, and re-layouts: 4.31 us -> 0 us
  Pallas kernels: 59.8 us -> 58.3 us
    unnamed x8 -> x0, local copies, waits for them, and re-layouts: 4.31 us -> none
    pallas_call x2, Pallas kernels: 59.8 us -> 58.3 us  [the longest x1 57.1 us: body(): pl.pallas_call(exchange, out_shape=outs, in_specs=[hbm, hbm], out_specs=(...]
where the time goes in v2:
time: 59.1 us; the launch traced here: 59 us
  Pallas kernels  58.3 us (99%)
  between operations  0.64 us (1%)
    pallas_call x1, Pallas kernels, body(): pl.pallas_call(exchange, out_shape=outs, in_specs=[hbm, hbm], out_specs=(...  57.1 us
    pallas_call x1, Pallas kernels, body(): pl.pallas_call(emit, out_shape=outs, in_specs=[vmem, vmem, vmem], out_spe...  1.26 us

profile of v2, /device:TPU:1, one launch (start us, length us, event | category | flops | bytes accessed | tf_op | source)
XLA Modules:
  0.0 59.0 jit_solution(7502338689301232997)
XLA Ops:
  0.6 57.1 %exchange.1 = (bf16[2,448,512]{2,1,0:T(8,128)(2,1)S(1)}, bf16[2,448,512]{2,1,0:T(8,128)(2,1)S(1)}, bf16[2,16,448]{2,1,0:T(8,128)(2,1)S(1)}) custom-call(bf16[2,14,2,32,512]{4,3,2,1,0:T(8,128)(2,1)} %bitcast.3, bf16[2,128,512]{2,1,0:T(8,128)(2,1)} %p_hbm.1), custom_call_target="tpu_custom_call" | custom-call | tf_op jit(solution)/shard_map/exchange/pallas_call | solution.py:202
  57.7 1.3 %emit.1 = (bf16[2,448,512]{2,1,0:T(8,128)(2,1)}, bf16[2,448,512]{2,1,0:T(8,128)(2,1)}, bf16[2,16,448]{2,1,0:T(8,128)(2,1)}) custom-call(bf16[2,448,512]{2,1,0:T(8,128)(2,1)S(1)} %get-tuple-element.6.gate_in, bf16[2,448,512]{2,1,0:T(8,128)(2,1)S(1)} %get-tuple-element.7.up_in, bf16[2,16,448]{2,1,0:T(8,128)(2,1)S(1)} %get-tuple-element.8.hid_in), custom_call_target="tpu_custom_call" | custom-call | tf_op jit(solution)/shard_map/emit/pallas_call | solution.py:234

commit v3 on v2

--- a/solution.py
+++ b/solution.py
@@ -12,7 +12,11 @@
 HB = B // 2
 J = L * B
 T = 128
-NY, NX = 4, 2
+NY, NX, NZ = 4, 2, 8
+TURN = 25
+GROUP = 4
+EARLY = 24
+BEFORE = 6
 TC = T // (NY * NX)
 PITCH = C + 1
 LANES = 128
@@ -27,23 +31,28 @@
 ):
     me = lax.axis_index("row")
     col = lax.axis_index("col")
-    xh, y = col // NY, col % NY
-
-    for gu in range(2):
-        for l in range(L):
-            q = gu * L + l
-            pltpu.make_async_copy(x_hbm.at[l, :, gu], xs.at[pl.ds(q * HB, HB)], load_sem.at[q]).start()
+    xh, y = lax.div(col, NY), lax.rem(col, NY)
+    xl, z, core = lax.div(me, 2 * NZ), lax.rem(lax.div(me, 2), NZ), lax.rem(me, 2)
+
+    def moved(step, sign):
+        turn = lax.rem(step * TURN, R)
+        dx, dz, dc = lax.div(turn, 2 * NZ), lax.rem(lax.div(turn, 2), NZ), lax.rem(turn, 2)
+        there = lax.rem(z + NZ + sign * dz, NZ)
+        return lax.rem(xl + dx, 2) * (2 * NZ) + there * 2 + lax.rem(core + dc, 2)
+
+    for q in range(2 * L):
+        pltpu.make_async_copy(x_hbm.at[q % L, :, q // L], xs.at[pl.ds(q * HB, HB)], load_sem.at[q]).start()
     pltpu.make_async_copy(p_hbm, pv, p_sem).start()
 
     barrier = pltpu.get_barrier_semaphore()
 
     def hello(i, _):
-        pl.semaphore_signal(barrier, inc=1, device_id={"row": (me + i) % R}, device_id_type=MESH)
+        pl.semaphore_signal(barrier, inc=1, device_id={"row": lax.rem(me + i, R)}, device_id_type=MESH)
         return _
 
     lax.fori_loop(1, R, hello, 0)
     for dy in range(1, NY):
-        pl.semaphore_signal(barrier, inc=1, device_id={"col": xh * NY + (y + dy) % NY}, device_id_type=MESH)
+        pl.semaphore_signal(barrier, inc=1, device_id={"col": xh * NY + lax.rem(y + dy, NY)}, device_id_type=MESH)
     partner = (1 - xh) * NY + y
     pl.semaphore_signal(barrier, inc=1, device_id={"col": partner}, device_id_type=MESH)
 
@@ -57,6 +66,26 @@
     for k in range(C):
         for c in range(TILES):
             msg[k, :, pl.ds(c * LANES, LANES)] = spread[c, pl.ds(k, J, stride=PITCH), :].astype(jnp.bfloat16)
+
+    pl.semaphore_wait(barrier, R - 1 + NY)
+
+    def start_weights(s, _):
+        to = moved(s, 1)
+        pltpu.make_async_remote_copy(
+            src_ref=msg.at[to], dst_ref=got.at[me], send_sem=w_send, recv_sem=w_recv.at[lax.div(s - 1, GROUP)],
+            device_id={"row": to}, device_id_type=MESH,
+        ).start()
+        return _
+
+    def start_hidden(s, _):
+        to = moved(s, 1)
+        pltpu.make_async_remote_copy(
+            src_ref=hsend.at[to], dst_ref=hgot.at[me], send_sem=h_send, recv_sem=h_recv,
+            device_id={"row": to}, device_id_type=MESH,
+        ).start()
+        return _
+
+    lax.fori_loop(1, EARLY + 1, start_weights, 0)
 
     pltpu.make_async_copy(p_hbm, pv, p_sem).wait()
     for l in range(L):
@@ -70,36 +99,12 @@
                     t = (a * NY + b) * TC
                     part[b, a, l, :, pl.ds(gu * HALFW, ROWS)] = proj[t:t + TC]
 
-    pl.semaphore_wait(barrier, R - 1 + NY)
-
-    def weights(i):
-        to = (me + i) % R
-        return pltpu.make_async_remote_copy(
-            src_ref=msg.at[to], dst_ref=got.at[me], send_sem=w_send.at[i], recv_sem=w_recv.at[me],
-            device_id={"row": to}, device_id_type=MESH,
-        )
-
-    def hiddens(i):
-        to = (me + i) % R
-        return pltpu.make_async_remote_copy(
-            src_ref=hsend.at[to], dst_ref=hgot.at[me], send_sem=h_send.at[i], recv_sem=h_recv.at[me],
-            device_id={"row": to}, device_id_type=MESH,
-        )
-
-    def start_weights(i, _):
-        weights(i).start()
-        return _
-
-    def phase_a(dy):
-        to = (y + dy) % NY
-        return pltpu.make_async_remote_copy(
-            src_ref=part.at[to], dst_ref=in_a.at[dy - 1], send_sem=a_send.at[dy - 1], recv_sem=a_recv.at[dy - 1],
+    for dy in range(1, NY):
+        to = lax.rem(y + dy, NY)
+        pltpu.make_async_remote_copy(
+            src_ref=part.at[to], dst_ref=in_a.at[dy - 1], send_sem=a_send, recv_sem=a_recv,
             device_id={"col": xh * NY + to}, device_id_type=MESH,
-        )
-
-    for dy in range(1, NY):
-        phase_a(dy).start()
-    lax.fori_loop(1, R, start_weights, 0)
+        ).start()
 
     def place(p, rows_of):
         for c in range(TILES):
@@ -110,15 +115,14 @@
 
     place(me, msg)
 
-    for dy in range(1, NY):
-        phase_a(dy).wait()
+    pltpu.make_async_copy(in_a, in_a, a_recv).wait()
     summed[...] = part[y] + in_a[0] + in_a[1] + in_a[2]
     phase_b = pltpu.make_async_remote_copy(
         src_ref=summed.at[1 - xh], dst_ref=in_b, send_sem=b_send, recv_sem=b_recv,
         device_id={"col": partner}, device_id_type=MESH,
     )
     phase_b.start()
-    phase_b.wait()
+    phase_b.wait_recv()
     total = summed[xh] + in_b[...]
     left, right = total[:, :, :HALFW], total[:, :, HALFW:]
     act = left / (1.0 + jnp.exp(-left)) * right
@@ -129,21 +133,22 @@
     for k in range(C):
         hsend[k] = hidt[pl.ds(k, 4, stride=C), :].astype(jnp.bfloat16)
 
-    def start_hidden(i, _):
-        hiddens(i).start()
-        return _
-
     lax.fori_loop(1, R, start_hidden, 0)
+    lax.fori_loop(EARLY + 1, R, start_weights, 0)
     hgot[me] = hsend[me]
 
-    for i in range(1, R):
-        hiddens(i).wait_send()
-    for i in range(1, R):
-        src = (me + i) % R
-        pltpu.make_async_remote_copy(
-            src_ref=hsend.at[0], dst_ref=hgot.at[src], send_sem=h_send.at[i], recv_sem=h_recv.at[src],
-            device_id={"row": src}, device_id_type=MESH,
-        ).wait_recv()
+    def arrived(s, _):
+        place(moved(s, -1), got)
+        return _
+
+    def group(g, _):
+        pltpu.make_async_copy(got.at[pl.ds(0, GROUP)], got.at[pl.ds(0, GROUP)], w_recv.at[g]).wait()
+        lax.fori_loop(g * GROUP + 1, g * GROUP + GROUP + 1, arrived, 0)
+        return _
+
+    whole = (R - 1) // GROUP
+    lax.fori_loop(0, BEFORE, group, 0)
+    pltpu.make_async_copy(hgot.at[pl.ds(0, R - 1)], hgot.at[pl.ds(0, R - 1)], h_recv).wait()
     for g in (3, 0, 1, 2):
         n = 2 if g == 3 else 4
         for p in range(R):
@@ -152,27 +157,20 @@
     flat = order[...].T
     for l in range(L):
         hid[l] = flat[l * TC:(l + 1) * TC, :ROWS].astype(jnp.bfloat16)
-
-    def arrived(i, _):
-        src = (me + R - i) % R
-        pltpu.make_async_remote_copy(
-            src_ref=msg.at[0], dst_ref=got.at[src], send_sem=w_send.at[i], recv_sem=w_recv.at[src],
-            device_id={"row": src}, device_id_type=MESH,
-        ).wait_recv()
-        place(src, got)
-        return _
-
-    lax.fori_loop(1, R, arrived, 0)
+    lax.fori_loop(BEFORE, whole, group, 0)
+    rest = R - 1 - whole * GROUP
+    pltpu.make_async_copy(got.at[pl.ds(0, rest)], got.at[pl.ds(0, rest)], w_recv.at[whole]).wait()
+    lax.fori_loop(whole * GROUP + 1, R, arrived, 0)
+
     for l in range(L):
         for c in range(TILES):
             gate[l, :, pl.ds(c * LANES, LANES)] = lined[l, c].astype(jnp.bfloat16)
             up[l, :, pl.ds(c * LANES, LANES)] = lined[L + l, c].astype(jnp.bfloat16)
 
-    def sent(i, _):
-        weights(i).wait_send()
-        return _
-
-    lax.fori_loop(1, R, sent, 0)
+    pltpu.make_async_copy(msg.at[pl.ds(0, R - 1)], msg.at[pl.ds(0, R - 1)], w_send).wait()
+    pltpu.make_async_copy(in_a, in_a, a_send).wait()
+    phase_b.wait_send()
+    pltpu.make_async_copy(hgot.at[pl.ds(0, R - 1)], hgot.at[pl.ds(0, R - 1)], h_send).wait()
 
 
 def emit(gate_in, up_in, hid_in, gate, up, hid, sems):
@@ -221,10 +219,10 @@
             pltpu.VMEM((R, 4, LANES), bf16),
             pltpu.VMEM((512, LANES), f32),
             dma((2 * L,)), dma,
-            dma((R,)), dma((R,)),
-            dma((NY - 1,)), dma((NY - 1,)),
+            dma, dma((-(-(R - 1) // GROUP),)),
             dma, dma,
-            dma((R,)), dma((R,)),
+            dma, dma,
+            dma, dma,
         ],
         compiler_params=pltpu.CompilerParams(
             collective_id=0, has_side_effects=True, vmem_limit_bytes=32 * 2**20

time: 59.1 us -> 54.1 us (0.915)
  Pallas kernels: 58.3 us -> 52.9 us
    pallas_call x1, Pallas kernels: 57.1 us -> 51.7 us  [body(): pl.pallas_call(exchange, out_shape=outs, in_specs=[hbm, hbm], out_specs=(...]
where the time goes in v3:
time: 54.1 us; the launch traced here: 53.5 us
  Pallas kernels  52.9 us (98%)
  between operations  0.64 us (1%)
    pallas_call x1, Pallas kernels, body(): pl.pallas_call(exchange, out_shape=outs, in_specs=[hbm, hbm], out_specs=(...  51.7 us
    pallas_call x1, Pallas kernels, body(): pl.pallas_call(emit, out_shape=outs, in_specs=[vmem, vmem, vmem], out_spe...  1.26 us

profile of v3, /device:TPU:1, one launch (start us, length us, event | category | flops | bytes accessed | tf_op | source)
XLA Modules:
  0.0 53.5 jit_solution(14650421754670743278)
XLA Ops:
  0.6 51.7 %exchange.1 = (bf16[2,448,512]{2,1,0:T(8,128)(2,1)S(1)}, bf16[2,448,512]{2,1,0:T(8,128)(2,1)S(1)}, bf16[2,16,448]{2,1,0:T(8,128)(2,1)S(1)}) custom-call(bf16[2,14,2,32,512]{4,3,2,1,0:T(8,128)(2,1)} %bitcast.3, bf16[2,128,512]{2,1,0:T(8,128)(2,1)} %p_hbm.1), custom_call_target="tpu_custom_call" | custom-call | tf_op jit(solution)/shard_map/exchange/pallas_call | solution.py:200
  52.3 1.3 %emit.1 = (bf16[2,448,512]{2,1,0:T(8,128)(2,1)}, bf16[2,448,512]{2,1,0:T(8,128)(2,1)}, bf16[2,16,448]{2,1,0:T(8,128)(2,1)}) custom-call(bf16[2,448,512]{2,1,0:T(8,128)(2,1)S(1)} %get-tuple-element.6.gate_in, bf16[2,448,512]{2,1,0:T(8,128)(2,1)S(1)} %get-tuple-element.7.up_in, bf16[2,16,448]{2,1,0:T(8,128)(2,1)S(1)} %get-tuple-element.8.hid_in), custom_call_target="tpu_custom_call" | custom-call | tf_op jit(solution)/shard_map/emit/pallas_call | solution.py:232

commit v4 on v3

v4 whole, which is shorter than its diff:
```python
import functools

import jax
import jax.numpy as jnp
from jax import lax
from jax.experimental import pallas as pl
from jax.experimental.pallas import tpu as pltpu
from jax.sharding import PartitionSpec as P

MESH = pl.DeviceIdType.MESH
L, C, R, B, W = 2, 32, 32, 28, 512
HB = B // 2
J = L * B
T = 128
NY, NX, NZ = 4, 2, 8
FIRST = (2, 14, 19, 31, 3, 15, 18, 30)
ORDER = FIRST + tuple(n for n in (25 * s % 32 for s in range(1, 32)) if n not in FIRST)
NEAR = 11
SENDNEAR = len(FIRST)
GROUP = 4
EARLY = 22
BEFORE = 5
AHEAD = 2
LIMIT = 24
BONUS = (8, 0, 0, 0, 0, 0, 0, 0)
TC = T // (NY * NX)
PITCH = C + 1
LANES = 128
TILES = W // LANES
HALFW = 512
ROWS = C * HB


def plan(z, bonus):
    def rank(n):
        return n - (bonus[(z + ORDER[n] // 2) % NZ] if n >= LIMIT else 0)

    return [ORDER[n] + R * (n // GROUP) for n in sorted(range(R - 1), key=rank)]


def exchange(
    x_hbm, p_hbm, lined, hid, xs, pv, spread, msg, got, stage, part, in_a, summed, in_b, hidt, hsend, hgot, order,
    load_sem, p_sem, w_send, w_recv, a_send, a_recv, b_send, b_recv, h_send, h_recv, near_sem, far_sem,
):
    me = lax.axis_index("row")
    col = lax.axis_index("col")
    xh, y = lax.div(col, NY), lax.rem(col, NY)
    xl, z, core = lax.div(me, 2 * NZ), lax.rem(lax.div(me, 2), NZ), lax.rem(me, 2)

    def moved(turn, sign):
        dx, dz, dc = lax.div(turn, 2 * NZ), lax.rem(lax.div(turn, 2), NZ), lax.rem(turn, 2)
        there = lax.rem(z + NZ + sign * dz, NZ)
        return lax.rem(xl + dx, 2) * (2 * NZ) + there * 2 + lax.rem(core + dc, 2)

    for q in range(2 * L):
        pltpu.make_async_copy(x_hbm.at[q % L, :, q // L], xs.at[pl.ds(q * HB, HB)], load_sem.at[q]).start()
    pltpu.make_async_copy(p_hbm, pv, p_sem).start()

    barrier = pltpu.get_barrier_semaphore()

    partner = (1 - xh) * NY + y
    for n in (n for n in ORDER if (n // 2 + 1) % NZ <= 2):
        pl.semaphore_signal(barrier, inc=1, device_id={"row": moved(n, 1)}, device_id_type=MESH)
    pl.semaphore_signal(barrier, inc=1, device_id={"col": partner}, device_id_type=MESH)
    for dy in range(1, NY):
        pl.semaphore_signal(barrier, inc=1, device_id={"col": xh * NY + lax.rem(y + dy, NY)}, device_id_type=MESH)

    for q in range(2 * L):
        pltpu.make_async_copy(x_hbm.at[q % L, :, q // L], xs.at[pl.ds(q * HB, HB)], load_sem.at[q]).wait()
        for i in range(HB):
            j = q * HB + i
            rows = xs[j].astype(jnp.float32)
            for c in range(TILES):
                spread[c, pl.ds(j * PITCH, C), :] = rows[:, c * LANES:(c + 1) * LANES]
    def build(k):
        for c in range(TILES):
            msg[k, :, pl.ds(c * LANES, LANES)] = spread[c, pl.ds(k, J, stride=PITCH), :].astype(jnp.bfloat16)

    plans = [plan(n, BONUS) for n in range(NZ)]

    def choice(n):
        options = [p[n] for p in plans]
        code = jnp.int32(options[0])
        for at, option in enumerate(options):
            if option != options[0]:
                code = jnp.where(z == at, jnp.int32(option), code)
        return moved(lax.rem(code, R), 1), lax.div(code, R)

    chosen = [choice(n) for n in range(R - 1)]

    def start_weights(n):
        to, which = chosen[n]
        pltpu.make_async_remote_copy(
            src_ref=msg.at[to], dst_ref=got.at[me], send_sem=w_send, recv_sem=w_recv.at[which],
            device_id={"row": to}, device_id_type=MESH,
        ).start()

    def start_hidden(n):
        to, _ = chosen[n]
        pltpu.make_async_remote_copy(
            src_ref=hsend.at[to], dst_ref=hgot.at[me], send_sem=h_send, recv_sem=h_recv,
            device_id={"row": to}, device_id_type=MESH,
        ).start()

    def send(first, last):
        for n in range(first, last):
            if n + AHEAD < R - 1:
                build(chosen[n + AHEAD][0])
            start_weights(n)

    def tell(sem, steps):
        for turn in (2 * steps, 2 * (NZ - steps)):
            pl.semaphore_signal(sem, inc=1, device_id={"row": moved(turn, 1)}, device_id_type=MESH)

    for n in range(AHEAD):
        build(chosen[n][0])
    pl.semaphore_wait(barrier, NEAR + NY)
    tell(near_sem, 1)
    send(0, SENDNEAR)
    pl.semaphore_wait(near_sem, 2)
    tell(far_sem, 2)
    pltpu.make_async_copy(p_hbm, pv, p_sem).wait()
    for l in range(L):
        for gu in range(2):
            rows = xs[pl.ds((gu * L + l) * HB, HB)].reshape(ROWS, W)
            proj = lax.dot_general(
                pv[l], rows, (((1,), (1,)), ((), ())), preferred_element_type=jnp.float32
            )
            for a in range(NX):
                for b in range(NY):
                    t = (a * NY + b) * TC
                    part[l, b, a, :, pl.ds(gu * HALFW, ROWS)] = proj[t:t + TC]
        for dy in range(1, NY):
            to = lax.rem(y + dy, NY)
            pltpu.make_async_remote_copy(
                src_ref=part.at[l, to], dst_ref=in_a.at[l, dy - 1], send_sem=a_send, recv_sem=a_recv.at[l],
                device_id={"col": xh * NY + to}, device_id_type=MESH,
            ).start()
    for n in range(EARLY + AHEAD, R - 1):
        build(chosen[n][0])
    build(me)
    pl.semaphore_wait(far_sem, 2)
    send(SENDNEAR, EARLY)

    def place(p, rows_of):
        for c in range(TILES):
            stage[c] = rows_of[p, :, pl.ds(c * LANES, LANES)].astype(jnp.float32)
        for c in range(TILES):
            for q in range(2 * L):
                lined[q, c, pl.ds(p * HB, HB), :] = stage[c, pl.ds(q * HB, HB), :]

    place(me, msg)

    phase_b = []
    for l in range(L):
        pltpu.make_async_copy(in_a.at[l], in_a.at[l], a_recv.at[l]).wait()
        summed[l] = part[l, y] + in_a[l, 0] + in_a[l, 1] + in_a[l, 2]
        phase_b.append(pltpu.make_async_remote_copy(
            src_ref=summed.at[l, 1 - xh], dst_ref=in_b.at[l], send_sem=b_send.at[l], recv_sem=b_recv.at[l],
            device_id={"col": partner}, device_id_type=MESH,
        ))
        phase_b[l].start()
    act = []
    for l in range(L):
        phase_b[l].wait_recv()
        total = summed[l, xh] + in_b[l]
        left, right = total[:, :HALFW], total[:, HALFW:]
        act.append(left / (1.0 + jnp.exp(-left)) * right)
    stacked = jnp.concatenate(
        [act[l][:, g * LANES:(g + 1) * LANES] for g in range(4) for l in range(L)], axis=0
    )
    hidt[...] = stacked.T
    for k in range(C):
        hsend[k] = hidt[pl.ds(k, 4, stride=C), :].astype(jnp.bfloat16)

    for n in range(R - 1):
        start_hidden(n)
    for n in range(EARLY, R - 1):
        start_weights(n)
    hgot[me] = hsend[me]

    def groups(first, last):
        for g in range(first, last):
            turns = ORDER[g * GROUP:(g + 1) * GROUP]
            many = pl.ds(0, len(turns))
            pltpu.make_async_copy(got.at[many], got.at[many], w_recv.at[g]).wait()

            def arrived(i, _):
                turn = jnp.int32(turns[0])
                for n, other in enumerate(turns[1:]):
                    turn = jnp.where(i > n, jnp.int32(other), turn)
                place(moved(turn, -1), got)
                return _

            lax.fori_loop(0, len(turns), arrived, 0)

    groups(0, BEFORE)
    pltpu.make_async_copy(hgot.at[pl.ds(0, R - 1)], hgot.at[pl.ds(0, R - 1)], h_recv).wait()
    for g in (3, 0, 1, 2):
        n = 2 if g == 3 else 4
        for p in range(R):
            piece = hgot[p].astype(jnp.float32)
            order[pl.ds(p * HB + 4 * g, n), :] = pltpu.roll(piece, (LANES - 32 * g) % LANES, 1)[:n]
    flat = order[...].T
    for l in range(L):
        hid[l] = flat[l * TC:(l + 1) * TC, :ROWS].astype(jnp.bfloat16)
    groups(BEFORE, -(-(R - 1) // GROUP))

    pltpu.make_async_copy(msg.at[pl.ds(0, R - 1)], msg.at[pl.ds(0, R - 1)], w_send).wait()
    pltpu.make_async_copy(in_a, in_a, a_send).wait()
    for copy in phase_b:
        copy.wait_send()
    pltpu.make_async_copy(hgot.at[pl.ds(0, R - 1)], hgot.at[pl.ds(0, R - 1)], h_send).wait()


def emit(lined, hid_in, gate, up, hid, rows, sems):
    copies = [pltpu.make_async_copy(hid_in, hid, sems.at[2 * L])]
    copies[0].start()
    for q in range(2 * L):
        for c in range(TILES):
            rows[q, :, pl.ds(c * LANES, LANES)] = lined[q, c].astype(jnp.bfloat16)
        copies.append(pltpu.make_async_copy(rows.at[q], (gate, up)[q // L].at[q % L], sems.at[q]))
        copies[-1].start()
    for copy in copies:
        copy.wait()


def body(joined, probes):
    x = jnp.transpose(joined, (0, 2, 3, 1, 4)).reshape(L, HB, 2, C, W)
    hbm = pl.BlockSpec(memory_space=pltpu.HBM)
    vmem = pl.BlockSpec(memory_space=pltpu.VMEM)
    dma = pltpu.SemaphoreType.DMA
    f32, bf16 = jnp.float32, jnp.bfloat16
    outs = (
        jax.ShapeDtypeStruct((L, ROWS, W), bf16),
        jax.ShapeDtypeStruct((L, ROWS, W), bf16),
        jax.ShapeDtypeStruct((L, TC, ROWS), bf16),
    )
    x = pltpu.with_memory_space_constraint(x, pltpu.HBM)
    probes = pltpu.with_memory_space_constraint(probes, pltpu.HBM)
    held = pl.pallas_call(
        exchange,
        out_shape=(jax.ShapeDtypeStruct((2 * L, TILES, ROWS, LANES), f32), outs[2]),
        in_specs=[hbm, hbm],
        out_specs=(vmem, vmem),
        scratch_shapes=[
            pltpu.VMEM((J, C, W), bf16),
            pltpu.VMEM((L, T, W), bf16),
            pltpu.VMEM((TILES, J * PITCH, LANES), f32),
            pltpu.VMEM((C, J, W), bf16),
            pltpu.VMEM((R, J, W), bf16),
            pltpu.VMEM((TILES, J, LANES), f32),
            pltpu.VMEM((L, NY, NX, TC, 2 * HALFW), f32),
            pltpu.VMEM((L, NY - 1, NX, TC, 2 * HALFW), f32),
            pltpu.VMEM((L, NX, TC, 2 * HALFW), f32),
            pltpu.VMEM((L, TC, 2 * HALFW), f32),
            pltpu.VMEM((LANES, LANES), f32),
            pltpu.VMEM((C, 4, LANES), bf16),
            pltpu.VMEM((R, 4, LANES), bf16),
            pltpu.VMEM((512, LANES), f32),
            dma((2 * L,)), dma,
            dma, dma((-(-(R - 1) // GROUP),)),
            dma, dma((L,)),
            dma((L,)), dma((L,)),
            dma, dma,
            pltpu.SemaphoreType.REGULAR, pltpu.SemaphoreType.REGULAR,
        ],
        compiler_params=pltpu.CompilerParams(
            collective_id=0, has_side_effects=True, vmem_limit_bytes=32 * 2**20
        ),
        name="exchange",
    )(x, probes)
    return pl.pallas_call(
        emit,
        out_shape=outs,
        in_specs=[vmem, vmem],
        out_specs=(hbm, hbm, hbm),
        scratch_shapes=[pltpu.VMEM((2 * L, ROWS, W), bf16), dma((2 * L + 1,))],
        compiler_params=pltpu.CompilerParams(vmem_limit_bytes=4 * 2**20),
        name="emit",
    )(*held)


def solution(mesh):
    return jax.shard_map(
        body,
        mesh=mesh,
        in_specs=(P(None, None, "row", None, "col"), P(None, None, "col")),
        out_specs=(P(None, "row", "col"), P(None, "row", "col"), P(None, "col", "row")),
        check_vma=False,
    )
```

time: 54.1 us -> 52.4 us (0.969)
  the two profiles are of different devices: /device:TPU:1 before, /device:TPU:64 now
where the time goes in v4:
time: 52.4 us; the launch traced here: 52.3 us
  Pallas kernels  51.7 us (99%)
  between operations  0.64 us (1%)
    pallas_call x1, Pallas kernels, body(): pl.pallas_call(exchange, out_shape=(jax.ShapeDtypeStruct((2 * L, TILES, R...  50.3 us
    pallas_call x1, Pallas kernels, body(): pl.pallas_call(emit, out_shape=outs, in_specs=[vmem, vmem], out_specs=(hb...  1.33 us

profile of v4, /device:TPU:64, one launch (start us, length us, event | category | flops | bytes accessed | tf_op | source)
XLA Modules:
  0.0 52.3 jit_solution(13462736912618081371)
XLA Ops:
  0.6 50.3 %exchange.1 = (f32[4,4,448,128]{3,2,1,0:T(8,128)S(1)}, bf16[2,16,448]{2,1,0:T(8,128)(2,1)S(1)}) custom-call(bf16[2,14,2,32,512]{4,3,2,1,0:T(8,128)(2,1)} %bitcast.3, bf16[2,128,512]{2,1,0:T(8,128)(2,1)} %p_hbm.1), custom_call_target="tpu_custom_call" | custom-call | tf_op jit(solution)/shard_map/exchange/pallas_call | solution.py:241
  51.0 1.3 %emit.1 = (bf16[2,448,512]{2,1,0:T(8,128)(2,1)}, bf16[2,448,512]{2,1,0:T(8,128)(2,1)}, bf16[2,16,448]{2,1,0:T(8,128)(2,1)}) custom-call(f32[4,4,448,128]{3,2,1,0:T(8,128)S(1)} %get-tuple-element.5.lined, bf16[2,16,448]{2,1,0:T(8,128)(2,1)S(1)} %get-tuple-element.6.hid_in), custom_call_target="tpu_custom_call" | custom-call | tf_op jit(solution)/shard_map/emit/pallas_call | solution.py:273

commit v5 on v4

--- a/solution.py
+++ b/solution.py
@@ -13,13 +13,17 @@
 J = L * B
 T = 128
 NY, NX, NZ = 4, 2, 8
-FIRST = (2, 14, 19, 31, 3, 15, 18, 30)
-ORDER = FIRST + tuple(n for n in (25 * s % 32 for s in range(1, 32)) if n not in FIRST)
+FIRST = (2, 14, 19, 31)
+NEXT = (4, 12, 21, 29)
+ORDER = FIRST + NEXT + tuple(n for n in (25 * s % 32 for s in range(1, 32)) if n not in FIRST + NEXT)
 NEAR = 11
 SENDNEAR = len(FIRST)
+SENDNEXT = SENDNEAR + len(NEXT)
 GROUP = 4
 EARLY = 22
-BEFORE = 5
+MIDWAY = 5
+BEFORE = 6
+HIDDEN = (4, 3, 5, 2, 6, 1, 7)
 AHEAD = 2
 LIMIT = 24
 BONUS = (8, 0, 0, 0, 0, 0, 0, 0)
@@ -39,8 +43,8 @@
 
 
 def exchange(
-    x_hbm, p_hbm, lined, hid, xs, pv, spread, msg, got, stage, part, in_a, summed, in_b, hidt, hsend, hgot, order,
-    load_sem, p_sem, w_send, w_recv, a_send, a_recv, b_send, b_recv, h_send, h_recv, near_sem, far_sem,
+    x_hbm, p_hbm, lined, hid, xs, pv, spread, msg, got, stage, part, in_a, summed, in_b, hidt, hsend, hmid, hgot, order,
+    load_sem, p_sem, w_send, w_recv, a_send, a_recv, b_send, b_recv, h_send, h_recv, m_send, m_recv, near_sem, far_sem,
 ):
     me = lax.axis_index("row")
     col = lax.axis_index("col")
@@ -95,10 +99,20 @@
             device_id={"row": to}, device_id_type=MESH,
         ).start()
 
-    def start_hidden(n):
-        to, _ = chosen[n]
+    seat = xl * 2 + core
+
+    def start_hidden(dz):
+        there = lax.rem(z + dz, NZ)
         pltpu.make_async_remote_copy(
-            src_ref=hsend.at[to], dst_ref=hgot.at[me], send_sem=h_send, recv_sem=h_recv,
+            src_ref=hsend.at[there], dst_ref=hmid.at[z], send_sem=h_send, recv_sem=h_recv,
+            device_id={"row": moved(2 * dz, 1)}, device_id_type=MESH,
+        ).start()
+
+    def pass_hidden(turn):
+        to = moved(turn, 1)
+        other = lax.div(to, 2 * NZ) * 2 + lax.rem(to, 2)
+        pltpu.make_async_remote_copy(
+            src_ref=hmid.at[:, other], dst_ref=hgot.at[seat], send_sem=m_send, recv_sem=m_recv,
             device_id={"row": to}, device_id_type=MESH,
         ).start()
 
@@ -119,6 +133,7 @@
     send(0, SENDNEAR)
     pl.semaphore_wait(near_sem, 2)
     tell(far_sem, 2)
+    send(SENDNEAR, SENDNEXT)
     pltpu.make_async_copy(p_hbm, pv, p_sem).wait()
     for l in range(L):
         for gu in range(2):
@@ -140,7 +155,7 @@
         build(chosen[n][0])
     build(me)
     pl.semaphore_wait(far_sem, 2)
-    send(SENDNEAR, EARLY)
+    send(SENDNEXT, EARLY)
 
     def place(p, rows_of):
         for c in range(TILES):
@@ -171,13 +186,13 @@
     )
     hidt[...] = stacked.T
     for k in range(C):
-        hsend[k] = hidt[pl.ds(k, 4, stride=C), :].astype(jnp.bfloat16)
-
-    for n in range(R - 1):
-        start_hidden(n)
+        hsend[k // 2 % NZ, k // (2 * NZ) * 2 + k % 2] = hidt[pl.ds(k, 4, stride=C), :].astype(jnp.bfloat16)
+
+    for dz in HIDDEN:
+        start_hidden(dz)
     for n in range(EARLY, R - 1):
         start_weights(n)
-    hgot[me] = hsend[me]
+    hmid[z] = hsend[z]
 
     def groups(first, last):
         for g in range(first, last):
@@ -194,12 +209,17 @@
 
             lax.fori_loop(0, len(turns), arrived, 0)
 
-    groups(0, BEFORE)
-    pltpu.make_async_copy(hgot.at[pl.ds(0, R - 1)], hgot.at[pl.ds(0, R - 1)], h_recv).wait()
+    groups(0, MIDWAY)
+    pltpu.make_async_copy(hmid.at[pl.ds(0, NZ - 1)], hmid.at[pl.ds(0, NZ - 1)], h_recv).wait()
+    for turn in (1, 2 * NZ, 2 * NZ + 1):
+        pass_hidden(turn)
+    hgot[seat] = hmid[:, seat]
+    groups(MIDWAY, BEFORE)
+    pltpu.make_async_copy(hgot.at[pl.ds(0, 3)], hgot.at[pl.ds(0, 3)], m_recv).wait()
     for g in (3, 0, 1, 2):
         n = 2 if g == 3 else 4
         for p in range(R):
-            piece = hgot[p].astype(jnp.float32)
+            piece = hgot[p // (2 * NZ) * 2 + p % 2, p // 2 % NZ].astype(jnp.float32)
             order[pl.ds(p * HB + 4 * g, n), :] = pltpu.roll(piece, (LANES - 32 * g) % LANES, 1)[:n]
     flat = order[...].T
     for l in range(L):
@@ -210,7 +230,8 @@
     pltpu.make_async_copy(in_a, in_a, a_send).wait()
     for copy in phase_b:
         copy.wait_send()
-    pltpu.make_async_copy(hgot.at[pl.ds(0, R - 1)], hgot.at[pl.ds(0, R - 1)], h_send).wait()
+    pltpu.make_async_copy(hmid.at[pl.ds(0, NZ - 1)], hmid.at[pl.ds(0, NZ - 1)], h_send).wait()
+    pltpu.make_async_copy(hgot.at[pl.ds(0, 3)], hgot.at[pl.ds(0, 3)], m_send).wait()
 
 
 def emit(lined, hid_in, gate, up, hid, rows, sems):
@@ -255,13 +276,15 @@
             pltpu.VMEM((L, NX, TC, 2 * HALFW), f32),
             pltpu.VMEM((L, TC, 2 * HALFW), f32),
             pltpu.VMEM((LANES, LANES), f32),
-            pltpu.VMEM((C, 4, LANES), bf16),
-            pltpu.VMEM((R, 4, LANES), bf16),
+            pltpu.VMEM((NZ, 4, 4, LANES), bf16),
+            pltpu.VMEM((NZ, 4, 4, LANES), bf16),
+            pltpu.VMEM((4, NZ, 4, LANES), bf16),
             pltpu.VMEM((512, LANES), f32),
             dma((2 * L,)), dma,
             dma, dma((-(-(R - 1) // GROUP),)),
             dma, dma((L,)),
             dma((L,)), dma((L,)),
+            dma, dma,
             dma, dma,
             pltpu.SemaphoreType.REGULAR, pltpu.SemaphoreType.REGULAR,
         ],

time: 52.4 us -> 52 us (level)
  the two profiles are of different devices: /device:TPU:64 before, /device:TPU:33 now
where the time goes in v5:
time: 52 us; the launch traced here: 51.9 us
  Pallas kernels  51.2 us (98%)
  between operations  0.64 us (1%)
    pallas_call x1, Pallas kernels, body(): pl.pallas_call(exchange, out_shape=(jax.ShapeDtypeStruct((2 * L, TILES, R...  49.9 us
    pallas_call x1, Pallas kernels, body(): pl.pallas_call(emit, out_shape=outs, in_specs=[vmem, vmem], out_specs=(hb...  1.33 us

profile of v5, /device:TPU:33, one launch (start us, length us, event | category | flops | bytes accessed | tf_op | source)
XLA Modules:
  0.0 51.9 jit_solution(10324231675110045312)
XLA Ops:
  0.6 49.9 %exchange.1 = (f32[4,4,448,128]{3,2,1,0:T(8,128)S(1)}, bf16[2,16,448]{2,1,0:T(8,128)(2,1)S(1)}) custom-call(bf16[2,14,2,32,512]{4,3,2,1,0:T(8,128)(2,1)} %bitcast.3, bf16[2,128,512]{2,1,0:T(8,128)(2,1)} %p_hbm.1), custom_call_target="tpu_custom_call" | custom-call | tf_op jit(solution)/shard_map/exchange/pallas_call | solution.py:262
  50.5 1.3 %emit.1 = (bf16[2,448,512]{2,1,0:T(8,128)(2,1)}, bf16[2,448,512]{2,1,0:T(8,128)(2,1)}, bf16[2,16,448]{2,1,0:T(8,128)(2,1)}) custom-call(f32[4,4,448,128]{3,2,1,0:T(8,128)S(1)} %get-tuple-element.5.lined, bf16[2,16,448]{2,1,0:T(8,128)(2,1)S(1)} %get-tuple-element.6.hid_in), custom_call_target="tpu_custom_call" | custom-call | tf_op jit(solution)/shard_map/emit/pallas_call | solution.py:296

commit v6 on v5

--- a/solution.py
+++ b/solution.py
@@ -25,8 +25,9 @@
 BEFORE = 6
 HIDDEN = (4, 3, 5, 2, 6, 1, 7)
 AHEAD = 2
+CUTS = 2
 LIMIT = 24
-BONUS = (8, 0, 0, 0, 0, 0, 0, 0)
+BONUS = (4, 0, 0, 0, 0, 0, 0, 0)
 TC = T // (NY * NX)
 PITCH = C + 1
 LANES = 128
@@ -159,7 +160,7 @@
 
     def place(p, rows_of):
         for c in range(TILES):
-            stage[c] = rows_of[p, :, pl.ds(c * LANES, LANES)].astype(jnp.float32)
+            stage[c, pl.ds(0, J), :] = rows_of[p, :, pl.ds(c * LANES, LANES)].astype(jnp.float32)
         for c in range(TILES):
             for q in range(2 * L):
                 lined[q, c, pl.ds(p * HB, HB), :] = stage[c, pl.ds(q * HB, HB), :]
@@ -184,7 +185,7 @@
     stacked = jnp.concatenate(
         [act[l][:, g * LANES:(g + 1) * LANES] for g in range(4) for l in range(L)], axis=0
     )
-    hidt[...] = stacked.T
+    hidt[pl.ds(0, LANES), :] = stacked.T
     for k in range(C):
         hsend[k // 2 % NZ, k // (2 * NZ) * 2 + k % 2] = hidt[pl.ds(k, 4, stride=C), :].astype(jnp.bfloat16)
 
@@ -235,13 +236,17 @@
 
 
 def emit(lined, hid_in, gate, up, hid, rows, sems):
-    copies = [pltpu.make_async_copy(hid_in, hid, sems.at[2 * L])]
+    copies = [pltpu.make_async_copy(hid_in, hid, sems.at[2 * L * CUTS])]
     copies[0].start()
     for q in range(2 * L):
-        for c in range(TILES):
-            rows[q, :, pl.ds(c * LANES, LANES)] = lined[q, c].astype(jnp.bfloat16)
-        copies.append(pltpu.make_async_copy(rows.at[q], (gate, up)[q // L].at[q % L], sems.at[q]))
-        copies[-1].start()
+        for n in range(CUTS):
+            span = pl.ds(n * (ROWS // CUTS), ROWS // CUTS)
+            for c in range(TILES):
+                rows[q, span, pl.ds(c * LANES, LANES)] = lined[q, c, span].astype(jnp.bfloat16)
+            copies.append(pltpu.make_async_copy(
+                rows.at[q, span], (gate, up)[q // L].at[q % L, span], sems.at[q * CUTS + n]
+            ))
+            copies[-1].start()
     for copy in copies:
         copy.wait()
 
@@ -261,7 +266,7 @@
     probes = pltpu.with_memory_space_constraint(probes, pltpu.HBM)
     held = pl.pallas_call(
         exchange,
-        out_shape=(jax.ShapeDtypeStruct((2 * L, TILES, ROWS, LANES), f32), outs[2]),
+        out_shape=(jax.ShapeDtypeStruct((2 * L, TILES, ROWS + 8, LANES), f32), outs[2]),
         in_specs=[hbm, hbm],
         out_specs=(vmem, vmem),
         scratch_shapes=[
@@ -270,12 +275,12 @@
             pltpu.VMEM((TILES, J * PITCH, LANES), f32),
             pltpu.VMEM((C, J, W), bf16),
             pltpu.VMEM((R, J, W), bf16),
-            pltpu.VMEM((TILES, J, LANES), f32),
+            pltpu.VMEM((TILES, J + 8, LANES), f32),
             pltpu.VMEM((L, NY, NX, TC, 2 * HALFW), f32),
             pltpu.VMEM((L, NY - 1, NX, TC, 2 * HALFW), f32),
             pltpu.VMEM((L, NX, TC, 2 * HALFW), f32),
             pltpu.VMEM((L, TC, 2 * HALFW), f32),
-            pltpu.VMEM((LANES, LANES), f32),
+            pltpu.VMEM((2 * LANES, LANES), f32),
             pltpu.VMEM((NZ, 4, 4, LANES), bf16),
             pltpu.VMEM((NZ, 4, 4, LANES), bf16),
             pltpu.VMEM((4, NZ, 4, LANES), bf16),
@@ -298,7 +303,7 @@
         out_shape=outs,
         in_specs=[vmem, vmem],
         out_specs=(hbm, hbm, hbm),
-        scratch_shapes=[pltpu.VMEM((2 * L, ROWS, W), bf16), dma((2 * L + 1,))],
+        scratch_shapes=[pltpu.VMEM((2 * L, ROWS, W), bf16), dma((2 * L * CUTS + 1,))],
         compiler_params=pltpu.CompilerParams(vmem_limit_bytes=4 * 2**20),
         name="emit",
     )(*held)

time: 52 us -> 51.9 us (level)
  no operation moved by 1% of the time
where the time goes in v6:
time: 51.9 us; the launch traced here: 51.8 us
  Pallas kernels  51.1 us (98%)
  between operations  0.64 us (1%)
    pallas_call x1, Pallas kernels, body(): pl.pallas_call(exchange, out_shape=(jax.ShapeDtypeStruct((2 * L, TILES, R...  49.8 us
    pallas_call x1, Pallas kernels, body(): pl.pallas_call(emit, out_shape=outs, in_specs=[vmem, vmem], out_specs=(hb...  1.33 us

profile of v6, /device:TPU:33, one launch (start us, length us, event | category | flops | bytes accessed | tf_op | source)
XLA Modules:
  0.0 51.8 jit_solution(1663019098664111016)
XLA Ops:
  0.6 49.8 %exchange.1 = (f32[4,4,456,128]{3,2,1,0:T(8,128)S(1)}, bf16[2,16,448]{2,1,0:T(8,128)(2,1)S(1)}) custom-call(bf16[2,14,2,32,512]{4,3,2,1,0:T(8,128)(2,1)} %bitcast.3, bf16[2,128,512]{2,1,0:T(8,128)(2,1)} %p_hbm.1), custom_call_target="tpu_custom_call" | custom-call | tf_op jit(solution)/shard_map/exchange/pallas_call | solution.py:267
  50.4 1.3 %emit.1 = (bf16[2,448,512]{2,1,0:T(8,128)(2,1)}, bf16[2,448,512]{2,1,0:T(8,128)(2,1)}, bf16[2,16,448]{2,1,0:T(8,128)(2,1)}) custom-call(f32[4,4,456,128]{3,2,1,0:T(8,128)S(1)} %get-tuple-element.5.lined, bf16[2,16,448]{2,1,0:T(8,128)(2,1)S(1)} %get-tuple-element.6.hid_in), custom_call_target="tpu_custom_call" | custom-call | tf_op jit(solution)/shard_map/emit/pallas_call | solution.py:301

commit v7 on v6

--- a/solution.py
+++ b/solution.py
@@ -14,7 +14,7 @@
 T = 128
 NY, NX, NZ = 4, 2, 8
 FIRST = (2, 14, 19, 31)
-NEXT = (4, 12, 21, 29)
+NEXT = (12, 29, 4, 21)
 ORDER = FIRST + NEXT + tuple(n for n in (25 * s % 32 for s in range(1, 32)) if n not in FIRST + NEXT)
 NEAR = 11
 SENDNEAR = len(FIRST)
@@ -27,7 +27,7 @@
 AHEAD = 2
 CUTS = 2
 LIMIT = 24
-BONUS = (4, 0, 0, 0, 0, 0, 0, 0)
+BONUS = (4, 3, 0, 0, 0, 0, 0, 0)
 TC = T // (NY * NX)
 PITCH = C + 1
 LANES = 128
@@ -130,11 +130,14 @@
     for n in range(AHEAD):
         build(chosen[n][0])
     pl.semaphore_wait(barrier, NEAR + NY)
-    tell(near_sem, 1)
+    for side, turn in enumerate((2, 2 * (NZ - 1))):
+        pl.semaphore_signal(near_sem.at[side], inc=1, device_id={"row": moved(turn, 1)}, device_id_type=MESH)
     send(0, SENDNEAR)
-    pl.semaphore_wait(near_sem, 2)
+    pl.semaphore_wait(near_sem.at[0], 1)
+    send(SENDNEAR, SENDNEAR + 2)
+    pl.semaphore_wait(near_sem.at[1], 1)
     tell(far_sem, 2)
-    send(SENDNEAR, SENDNEXT)
+    send(SENDNEAR + 2, SENDNEXT)
     pltpu.make_async_copy(p_hbm, pv, p_sem).wait()
     for l in range(L):
         for gu in range(2):
@@ -291,7 +294,7 @@
             dma((L,)), dma((L,)),
             dma, dma,
             dma, dma,
-            pltpu.SemaphoreType.REGULAR, pltpu.SemaphoreType.REGULAR,
+            pltpu.SemaphoreType.REGULAR((2,)), pltpu.SemaphoreType.REGULAR,
         ],
         compiler_params=pltpu.CompilerParams(
             collective_id=0, has_side_effects=True, vmem_limit_bytes=32 * 2**20

time: 51.9 us -> 51.6 us (level)
  the two profiles are of different devices: /device:TPU:33 before, /device:TPU:1 now
where the time goes in v7:
time: 51.6 us; the launch traced here: 50.9 us
  Pallas kernels  50.3 us (97%)
  between operations  0.64 us (1%)
    pallas_call x1, Pallas kernels, body(): pl.pallas_call(exchange, out_shape=(jax.ShapeDtypeStruct((2 * L, TILES, R...  49 us
    pallas_call x1, Pallas kernels, body(): pl.pallas_call(emit, out_shape=outs, in_specs=[vmem, vmem], out_specs=(hb...  1.33 us

profile of v7, /device:TPU:1, one launch (start us, length us, event | category | flops | bytes accessed | tf_op | source)
XLA Modules:
  0.0 50.9 jit_solution(14598297577723897972)
XLA Ops:
  0.6 49.0 %exchange.1 = (f32[4,4,456,128]{3,2,1,0:T(8,128)S(1)}, bf16[2,16,448]{2,1,0:T(8,128)(2,1)S(1)}) custom-call(bf16[2,14,2,32,512]{4,3,2,1,0:T(8,128)(2,1)} %bitcast.3, bf16[2,128,512]{2,1,0:T(8,128)(2,1)} %p_hbm.1), custom_call_target="tpu_custom_call" | custom-call | tf_op jit(solution)/shard_map/exchange/pallas_call | solution.py:270
  49.6 1.3 %emit.1 = (bf16[2,448,512]{2,1,0:T(8,128)(2,1)}, bf16[2,448,512]{2,1,0:T(8,128)(2,1)}, bf16[2,16,448]{2,1,0:T(8,128)(2,1)}) custom-call(f32[4,4,456,128]{3,2,1,0:T(8,128)S(1)} %get-tuple-element.5.lined, bf16[2,16,448]{2,1,0:T(8,128)(2,1)S(1)} %get-tuple-element.6.hid_in), custom_call_target="tpu_custom_call" | custom-call | tf_op jit(solution)/shard_map/emit/pallas_call | solution.py:304
